TPU v7x, 32 devices: a whole 2x2x4 slice. The times are simulated.
32 devices in a mesh: dp: 16 (over z, y, core), expert: 2 (over x).
Axes of the slice: x: 2, y: 2, z: 4, core: 2. Of those that a mesh axis runs over, the one named last changes fastest.
Arguments:
- tokens: bfloat16 [256, 6144], P('dp', 'expert'), may hold values from -6 to 6
- expert_ids: int32 [256, 2], P('dp'), may hold values from 0 to 7, all different within a row; in each aligned block of 16 rows (0 to 15, 16 to 31, ...) at most 8 rows name the same one
- gate_probs: float32 [256, 2], P('dp'), may hold values from 0.1 to 1
- w_gate: bfloat16 [8, 6144, 8192], P('expert', None, 'dp'), may hold values from -0.078125 to 0.078125
- w_up: bfloat16 [8, 6144, 8192], P('expert', None, 'dp'), may hold values from -0.078125 to 0.078125
- w_down_t: bfloat16 [8, 6144, 8192], P('expert', 'dp'), may hold values from -0.0625 to 0.0625
Outputs:
- mixed: bfloat16 [256, 6144], P('dp', 'expert')
Inputs may be any that keep to these rules, and one draw needn't show every extreme that they name: `expert_ids`: each row names 2 different experts. Among the 16 rows of one index of dp no expert is named more than 8 times, a bound that some block reaches.
All inputs are finite; a program needn't handle non-finite values.
Results may differ from a plain program's by a relative error of at most 0.0057.
Values may be sent and summed in bfloat16 or wider, within the bound.
A program may use at most 128 MiB of HBM per device.

v0:
```python
import jax
import jax.numpy as jnp
from jax import lax
from jax.sharding import PartitionSpec as P


def assignments(expert_ids, experts, capacity):
    flat = expert_ids.reshape(-1)
    onehot = (flat[:, None] == jnp.arange(experts, dtype=jnp.int32)[None, :]).astype(jnp.int32)
    earlier = jnp.cumsum(onehot, axis=0) - onehot
    position = jnp.sum(earlier * onehot, axis=1).reshape(expert_ids.shape)
    expert_hit = (
        expert_ids[:, :, None] == jnp.arange(experts, dtype=jnp.int32)[None, None, :]
    ).astype(jnp.float32)
    slot_hit = (
        position[:, :, None] == jnp.arange(capacity, dtype=jnp.int32)[None, None, :]
    ).astype(jnp.float32)
    return (expert_hit, slot_hit)


def per_device(tokens, expert_ids, gate_probs, w_gate, w_up, w_down_t):
    local_experts = w_gate.shape[0]
    expert_count = lax.axis_size("expert")
    dp_count = lax.axis_size("dp")
    experts = local_experts * expert_count
    capacity = tokens.shape[0] // 2
    expert_hit, slot_hit = assignments(expert_ids, experts, capacity)
    dispatch_map = jnp.einsum("tke,tkc->ect", expert_hit, slot_hit).astype(jnp.bfloat16)
    combine_map = jnp.einsum(
        "tk,tke,tkc->tec", gate_probs, expert_hit, slot_hit, precision=lax.Precision.HIGHEST
    )
    slots = jnp.einsum(
        "ect,td->ecd", dispatch_map, tokens, preferred_element_type=jnp.float32
    ).astype(jnp.bfloat16)
    arrived = lax.all_to_all(slots, "expert", split_axis=0, concat_axis=2, tiled=True)
    piece = lax.all_gather(arrived, "dp", axis=1, tiled=True)
    gate = jnp.einsum("erd,edf->erf", piece, w_gate, preferred_element_type=jnp.float32)
    up = jnp.einsum("erd,edf->erf", piece, w_up, preferred_element_type=jnp.float32)
    hidden = (jax.nn.silu(gate) * up).astype(jnp.bfloat16)
    partial_out = jnp.einsum(
        "erf,edf->erd",
        lax.all_gather(hidden, "dp", axis=2, tiled=True),
        w_down_t,
        preferred_element_type=jnp.float32,
    )
    results = partial_out.astype(jnp.bfloat16).reshape(
        local_experts, dp_count, capacity, w_down_t.shape[1]
    )
    results = lax.all_to_all(results, "dp", split_axis=1, concat_axis=3, tiled=True)
    results = results.reshape(local_experts, capacity, results.shape[3])
    slice_width = tokens.shape[1]
    outgoing = results.reshape(local_experts, capacity, expert_count, slice_width)
    returned = lax.all_to_all(outgoing, "expert", split_axis=2, concat_axis=0, tiled=True)
    returned = returned.reshape(experts, capacity, slice_width)
    mixed = jnp.einsum(
        "tec,ecd->td", combine_map, returned.astype(jnp.float32), precision=lax.Precision.HIGHEST
    )
    return mixed.astype(jnp.bfloat16)


def solution(mesh):
    placed = (
        P("dp", "expert"),
        P("dp", None),
        P("dp", None),
        P("expert", None, "dp"),
        P("expert", None, "dp"),
        P("expert", "dp", None),
    )
    return jax.shard_map(
        per_device, mesh=mesh, in_specs=placed, out_specs=P("dp", "expert"), check_vma=False
    )
```

profile of v0, /device:TPU:0, one launch (start us, length us, event | category | flops | bytes accessed | tf_op | source)
XLA Modules:
  0.0 233.5 jit_solution(2106220213072693453)
XLA Ops:
  6.5 0.8 copy.17
  7.3 0.1 eq.46
  7.5 0.2 select_reduce_fusion
  7.8 0.3 fusion.3
  8.1 0.1 copy.20
  8.2 0.2 convolution_convert_fusion
  8.5 10.6 %all_to_all.48 = bf16[8,8,3072]{2,1,0:T(8,128)(2,1)S(1)} all-to-all(bf16[8,8,3072]{2,1,0:T(8,128)(2,1)S(1)} %convolution_convert_fusion), channel_id=1, replica_groups=mesh['dp'=16,'expert'=2] {'expert'}, dimensions={0} | all-to-all | bytes 786432 | tf_op jit(solution)/shard_map/all_to_all | solution.py:35
  19.1 0.8 copy.21
  19.9 62.0 %all-gather.3.cloned.1.call-done = bf16[4,128,6144]{2,1,0:T(8,128)(2,1)} async-done(((bf16[4,8,6144]{2,1,0:T(8,128)(2,1)}), bf16[4,128,6144]{2,1,0:T(8,128)(2,1)}) %all-gather.3.cloned.1.call-update) | async-done | bytes 6291472 | tf_op jit(solution)/shard_map/all_gather | solution.py:36
  81.9 11.9 %fusion.16 = f32[4,128,512]{2,1,0:T(8,128)S(1)} fusion(bf16[4,128,6144]{2,1,0:T(8,128)(2,1)} %all-gather.3.cloned.1.call-done, bf16[4,6144,512]{2,1,0:T(8,128)(2,1)} %param.9), kind=kOutput, calls=%fused_computation.25 | convolution fusion | flops 3221225472 | bytes 32505856 | tf_op jit(solution)/shard_map/erd,edf->erf/dot_general | solution.py:37
  93.9 12.6 %fusion.1 = bf16[4,128,512]{2,1,0:T(8,128)(2,1)} fusion(bf16[4,128,6144]{2,1,0:T(8,128)(2,1)S(1)} %copy-done.2, bf16[4,6144,512]{2,1,0:T(8,128)(2,1)} %param.10, f32[4,128,512]{2,1,0:T(8,128)S(1)} %fusion.16), kind=kOutput, calls=%fused_computation.4 | convolution fusion | flops 3222798336 | bytes 33030144 | tf_op jit(solution)/shard_map/erd,edf->erf/dot_general | solution.py:38
  106.5 76.5 %all-gather.5.cloned.1.call-done = bf16[4,128,8192]{2,1,0:T(8,128)(2,1)} async-done(((bf16[4,128,512]{2,1,0:T(8,128)(2,1)}), bf16[4,128,8192]{2,1,0:T(8,128)(2,1)}) %all-gather.5.cloned.1.call-update) | async-done | bytes 8388624 | tf_op jit(solution)/shard_map/all_gather | solution.py:42
  183.0 14.5 %fusion.2 = bf16[4,16,8,384]{3,2,1,0:T(8,128)(2,1)S(1)} fusion(bf16[4,128,8192]{2,1,0:T(8,128)(2,1)} %all-gather.5.cloned.1.call-done, bf16[4,384,8192]{2,1,0:T(8,128)(2,1)} %param.11), kind=kOutput, calls=%fused_computation.6 | convolution fusion | flops 3221422080 | bytes 33947648 | tf_op jit(solution)/shard_map/erf,edf->erd/dot_general | solution.py:40
  197.5 0.8 copy.22
  198.3 3.6 %all-to-all-start.1 = ((bf16[4,16,8,384]{3,2,0,1:T(8,128)(2,1)}), bf16[4,16,8,384]{3,2,0,1:T(8,128)(2,1)S(1)}, u32[]{:S(2)}, u32[]{:S(2)}) async-start(bf16[4,16,8,384]{3,2,0,1:T(8,128)(2,1)} %copy.22), calls=%async_computation.1 | async-start | bytes 786432 | tf_op jit(solution)/shard_map/all_to_all | solution.py:49
  201.9 12.0 %all-to-all-done.1 = bf16[4,16,8,384]{3,2,0,1:T(8,128)(2,1)S(1)} async-done(((bf16[4,16,8,384]{3,2,0,1:T(8,128)(2,1)}), bf16[4,16,8,384]{3,2,0,1:T(8,128)(2,1)S(1)}, u32[]{:S(2)}, u32[]{:S(2)}) %all-to-all-start.1) | async-done | bytes 393248 | tf_op jit(solution)/shard_map/all_to_all | solution.py:49
  213.9 0.1 copy.23
  214.1 0.1 reshape_reshape.3
  214.2 0.8 copy.24
  215.0 3.5 %all-to-all-start.2 = ((bf16[4,8,2,3072]{3,1,0,2:T(8,128)(2,1)}), bf16[4,8,2,3072]{3,1,0,2:T(8,128)(2,1)S(1)}, u32[]{:S(2)}, u32[]{:S(2)}) async-start(bf16[4,8,2,3072]{3,1,0,2:T(8,128)(2,1)} %copy.24), calls=%async_computation.2 | async-start | bytes 786432 | tf_op jit(solution)/shard_map/all_to_all | solution.py:53
  218.5 0.4 fusion.6
  218.9 0.1 copy.26
  219.0 6.6 %all-to-all-done.2 = bf16[4,8,2,3072]{3,1,0,2:T(8,128)(2,1)S(1)} async-done(((bf16[4,8,2,3072]{3,1,0,2:T(8,128)(2,1)}), bf16[4,8,2,3072]{3,1,0,2:T(8,128)(2,1)S(1)}, u32[]{:S(2)}, u32[]{:S(2)}) %all-to-all-start.2) | async-done | bytes 393248 | tf_op jit(solution)/shard_map/all_to_all | solution.py:53
  225.6 1.1 fusion
  (16 shorter events, 0.4 us)
Async XLA Ops:
  6.5 1.7 copy-start
  6.5 75.4 %all-gather.3.cloned.1.call-start = ((), (), s32[]{:S(2)}) async-start(), calls=%async_computation.3 | async-start | bytes 6684672 | tf_op jit(solution)/shard_map/all_gather | solution.py:36
  19.9 163.1 %all-gather.5.cloned.1.call-start = ((), (), s32[]{:S(2)}) async-start(), calls=%async_computation.4 | async-start | bytes 8912896 | tf_op jit(solution)/shard_map/all_gather | solution.py:42
  81.9 11.9 %copy-start.2 = (bf16[4,128,6144]{2,1,0:T(8,128)(2,1)S(1)}, bf16[4,128,6144]{2,1,0:T(8,128)(2,1)}, u32[]{:S(2)}) copy-start(bf16[4,128,6144]{2,1,0:T(8,128)(2,1)} %all-gather.3.cloned.1.call-done) | copy-start | bytes 18874372
  93.9 132.8 %copy-start.1 = (bf16[16,3072]{1,0:T(8,128)(2,1)S(1)}, bf16[16,3072]{1,0:T(8,128)(2,1)}, u32[]{:S(2)}) copy-start(bf16[16,3072]{1,0:T(8,128)(2,1)} %param.6) | copy-start | bytes 294916
  106.4 95.4 %copy-start.3 = (f32[16,2]{0,1:T(2,128)S(1)}, f32[16,2]{0,1:T(2,128)}, u32[]{:S(2)}) copy-start(f32[16,2]{0,1:T(2,128)} %param.8) | copy-start | bytes 388
  198.3 15.7 %all-to-all-start.1 = ((bf16[4,16,8,384]{3,2,0,1:T(8,128)(2,1)}), bf16[4,16,8,384]{3,2,0,1:T(8,128)(2,1)S(1)}, u32[]{:S(2)}, u32[]{:S(2)}) async-start(bf16[4,16,8,384]{3,2,0,1:T(8,128)(2,1)} %copy.22), calls=%async_computation.1 | async-start | bytes 786432 | tf_op jit(solution)/shard_map/all_to_all | solution.py:49
  215.0 10.6 %all-to-all-start.2 = ((bf16[4,8,2,3072]{3,1,0,2:T(8,128)(2,1)}), bf16[4,8,2,3072]{3,1,0,2:T(8,128)(2,1)S(1)}, u32[]{:S(2)}, u32[]{:S(2)}) async-start(bf16[4,8,2,3072]{3,1,0,2:T(8,128)(2,1)} %copy.24), calls=%async_computation.2 | async-start | bytes 786432 | tf_op jit(solution)/shard_map/all_to_all | solution.py:53
Sparse Core Ops, SparseCore 0:
  20.0 61.8 all-gather.2
  106.6 76.3 all-gather.4
where the time goes:
time: 234 us
  waiting for transfers between devices  157 us (67%)
  matrix products  41 us (18%)
  between operations  13.5 us (6%)
  blocking collectives  10.6 us (5%)
  starting transfers between devices  7.06 us (3%)
  local copies, waits for them, and re-layouts  3.83 us (2%)
    all_gather x1, waiting for transfers between devices, per_device(): lax.all_gather(hidden, 'dp', axis=2, tiled=True)  76.5 us
    all_gather x1, waiting for transfers between devices, per_device(): piece = lax.all_gather(arrived, 'dp', axis=1, tiled=True)  62 us
    dot_general x1, matrix products, per_device(): jnp.einsum('erf,edf->erd', lax.all_gather(hidden, 'dp', axis=2, tiled=Tru...  14.5 us
    dot_general x1, matrix products, per_device(): jnp.einsum('erd,edf->erf', piece, w_up, preferred_element_type=jnp.float32)  12.6 us
    all_to_all x1, waiting for transfers between devices, per_device(): lax.all_to_all(results, 'dp', split_axis=1, concat_axis=3, tiled=True)  12 us
    dot_general x1, matrix products, per_device(): jnp.einsum('erd,edf->erf', piece, w_gate, preferred_element_type=jnp.floa...  11.9 us
    all_to_all x1, blocking collectives, per_device(): lax.all_to_all(slots, 'expert', split_axis=0, concat_axis=2, tiled=True)  10.6 us
    all_to_all x1, waiting for transfers between devices, per_device(): lax.all_to_all(outgoing, 'expert', split_axis=2, concat_axis=0, tiled=True)  6.61 us
  transfers between devices with their start and end apart: 4, of which 4 were waited for; matrix products, arithmetic and copies ran while one was open for 0% of the time, Pallas kernels for 0%

commit v1 on v0

--- a/solution.py
+++ b/solution.py
@@ -37,12 +37,38 @@
     gate = jnp.einsum("erd,edf->erf", piece, w_gate, preferred_element_type=jnp.float32)
     up = jnp.einsum("erd,edf->erf", piece, w_up, preferred_element_type=jnp.float32)
     hidden = (jax.nn.silu(gate) * up).astype(jnp.bfloat16)
-    partial_out = jnp.einsum(
+    size, mine, span = (lax.axis_size("dp"), lax.axis_index("dp"), hidden.shape[2])
+    forward = [(i, (i + 1) % size) for i in range(size)]
+    backward = [(i, (i - 1) % size) for i in range(size)]
+    halfway = size // 2
+    from_left = from_right = hidden
+    total = jnp.einsum(
         "erf,edf->erd",
-        lax.all_gather(hidden, "dp", axis=2, tiled=True),
-        w_down_t,
+        hidden,
+        lax.dynamic_slice_in_dim(w_down_t, mine * span, hidden.shape[2], axis=2),
         preferred_element_type=jnp.float32,
     )
+    for turn in range(1, halfway + 1):
+        from_left = lax.ppermute(from_left, "dp", forward)
+        if turn < size - halfway:
+            from_right = lax.ppermute(from_right, "dp", backward)
+            total = total + jnp.einsum(
+                "erf,edf->erd",
+                from_right,
+                lax.dynamic_slice_in_dim(
+                    w_down_t, (mine + turn) % size * span, from_right.shape[2], axis=2
+                ),
+                preferred_element_type=jnp.float32,
+            )
+        total = total + jnp.einsum(
+            "erf,edf->erd",
+            from_left,
+            lax.dynamic_slice_in_dim(
+                w_down_t, (mine - turn) % size * span, from_left.shape[2], axis=2
+            ),
+            preferred_element_type=jnp.float32,
+        )
+    partial_out = total
     results = partial_out.astype(jnp.bfloat16).reshape(
         local_experts, dp_count, capacity, w_down_t.shape[1]
     )

time: 234 us -> 253 us (1.081)
  starting transfers between devices: 7.06 us -> 61.6 us
  waiting for transfers between devices: 157 us -> 104 us
  matrix products: 41 us -> 58 us
    all_gather x1 -> x0, waiting for transfers between devices: 76.5 us -> none  [per_device(): lax.all_gather(hidden, 'dp', axis=2, tiled=True)]
    ppermute x0 -> x15, starting transfers between devices: none -> 47.6 us  [the longest x8 29.8 us: per_device(): from_left = lax.ppermute(from_left, 'dp', forward)]
    ppermute x0 -> x15, waiting for transfers between devices: none -> 23.3 us  [the longest x8 23.2 us: per_device(): from_left = lax.ppermute(from_left, 'dp', forward)]
    dot_general x1 -> x16, matrix products: 14.5 us -> 32.3 us  [the longest x8 16 us: per_device(): jnp.einsum('erf,edf->erd', from_left, lax.dynamic_slice_in_dim(w_down_t,...]
    all_to_all x1, starting transfers between devices: 3.55 us -> 10.6 us  [per_device(): lax.all_to_all(results, 'dp', split_axis=1, concat_axis=3, tiled=True)]
  transfers between devices with their start and end apart: 4 -> 18, of which waited for: 4 -> 11; matrix products, arithmetic and copies ran while one was open for 0% -> 12% of each run, Pallas kernels for 0% -> 0%
where the time goes in v1:
time: 253 us; the launch traced here: 252 us
  waiting for transfers between devices  104 us (41%)
  starting transfers between devices  61.6 us (24%)
  matrix products  58 us (23%)
  between operations  13.6 us (5%)
  blocking collectives  10.6 us (4%)
  local copies, waits for them, and re-layouts  3.88 us (2%)
    all_gather x1, waiting for transfers between devices, per_device(): piece = lax.all_gather(arrived, 'dp', axis=1, tiled=True)  62 us
    ppermute x8, starting transfers between devices, per_device(): from_left = lax.ppermute(from_left, 'dp', forward)  29.8 us
    ppermute x8, waiting for transfers between devices, per_device(): from_left = lax.ppermute(from_left, 'dp', forward)  23.2 us
    ppermute x7, starting transfers between devices, per_device(): from_right = lax.ppermute(from_right, 'dp', backward)  17.7 us
    dot_general x8, matrix products, per_device(): jnp.einsum('erf,edf->erd', from_left, lax.dynamic_slice_in_dim(w_down_t,...  16 us
    dot_general x7, matrix products, per_device(): jnp.einsum('erf,edf->erd', from_right, lax.dynamic_slice_in_dim(w_down_t,...  14.3 us
    all_to_all x1, waiting for transfers between devices, per_device(): lax.all_to_all(results, 'dp', split_axis=1, concat_axis=3, tiled=True)  12.1 us
    dot_general x1, matrix products, per_device(): jnp.einsum('erd,edf->erf', piece, w_gate, preferred_element_type=jnp.floa...  11.9 us
  transfers between devices with their start and end apart: 18, of which 11 were waited for; matrix products, arithmetic and copies ran while one was open for 12% of the time, Pallas kernels for 0%

profile of v1, /device:TPU:0, one launch (start us, length us, event | category | flops | bytes accessed | tf_op | source)
XLA Modules:
  0.0 252.0 jit_solution(17330850615361440236)
XLA Ops:
  8.5 10.6 %all_to_all.48 = bf16[8,8,3072]{2,1,0:T(8,128)(2,1)S(1)} all-to-all(bf16[8,8,3072]{2,1,0:T(8,128)(2,1)S(1)} %convolution_convert_fusion), channel_id=1, replica_groups=mesh['dp'=16,'expert'=2] {'expert'}, dimensions={0} | all-to-all | bytes 786432 | tf_op jit(solution)/shard_map/all_to_all | solution.py:35
  19.9 62.0 %all-gather.2.cloned.1.call-done = bf16[4,128,6144]{2,1,0:T(8,128)(2,1)} async-done(((bf16[4,8,6144]{2,1,0:T(8,128)(2,1)}), bf16[4,128,6144]{2,1,0:T(8,128)(2,1)}) %all-gather.2.cloned.1.call-update) | async-done | bytes 6291472 | tf_op jit(solution)/shard_map/all_gather | solution.py:36
  81.9 11.9 %fusion.114 = f32[4,128,512]{2,1,0:T(8,128)S(1)} fusion(bf16[4,128,6144]{2,1,0:T(8,128)(2,1)} %all-gather.2.cloned.1.call-done, bf16[4,6144,512]{2,1,0:T(8,128)(2,1)} %param.9), kind=kOutput, calls=%fused_computation.88 | convolution fusion | flops 3221225472 | bytes 32505856 | tf_op jit(solution)/shard_map/erd,edf->erf/dot_general | solution.py:37
  93.9 11.7 %fusion.78 = bf16[4,128,512]{2,1,0:T(8,128)(2,1)S(1)} fusion(bf16[4,128,6144]{2,1,0:T(8,128)(2,1)S(1)} %copy-done.2, bf16[4,6144,512]{2,1,0:T(8,128)(2,1)} %param.10, f32[4,128,512]{2,1,0:T(8,128)S(1)} %fusion.114), kind=kOutput, calls=%fused_computation.51 | convolution fusion | flops 3222798336 | bytes 33030144 | tf_op jit(solution)/shard_map/erd,edf->erf/dot_general | solution.py:38
  105.9 4.2 %collective-permute-start = (bf16[4,128,512]{2,1,0:T(8,128)(2,1)S(1)}, bf16[4,128,512]{2,1,0:T(8,128)(2,1)S(1)}, u32[]{:S(2)}, u32[]{:S(2)}) collective-permute-start(bf16[4,128,512]{2,1,0:T(8,128)(2,1)S(1)} %fusion.78), channel_id=1, source_target_pairs={{0,30},{2,0},{4,2},{6,4},{8,6},{10,8},{12,10},{14,12},{16,14},{18,... | collective-permute-start | bytes 1572872 | tf_op jit(solution)/shard_map/ppermute | solution.py:54
  112.1 5.0 %collective-permute-done.1 = bf16[4,128,512]{2,1,0:T(8,128)(2,1)S(1)} collective-permute-done((bf16[4,128,512]{2,1,0:T(8,128)(2,1)S(1)}, bf16[4,128,512]{2,1,0:T(8,128)(2,1)S(1)}, u32[]{:S(2)}, u32[]{:S(2)}) %collective-permute-start.1) | collective-permute-done | bytes 524320 | tf_op jit(solution)/shard_map/ppermute | solution.py:52
  118.0 3.4 %collective-permute-start.2 = (bf16[4,128,512]{2,1,0:T(8,128)(2,1)S(1)}, bf16[4,128,512]{2,1,0:T(8,128)(2,1)S(1)}, u32[]{:S(2)}, u32[]{:S(2)}) collective-permute-start(bf16[4,128,512]{2,1,0:T(8,128)(2,1)S(1)} %collective-permute-done), channel_id=1, source_target_pairs={{0,30},{2,0},{4,2},{6,4},{8,6},{10,8},{12,10},{14,12},{16,14},{18,... | collective-permute-start | bytes 1572872 | tf_op jit(solution)/shard_map/ppermute | solution.py:54
  125.5 2.9 %collective-permute-done.3 = bf16[4,128,512]{2,1,0:T(8,128)(2,1)S(1)} collective-permute-done((bf16[4,128,512]{2,1,0:T(8,128)(2,1)S(1)}, bf16[4,128,512]{2,1,0:T(8,128)(2,1)S(1)}, u32[]{:S(2)}, u32[]{:S(2)}) %collective-permute-start.3) | collective-permute-done | bytes 524320 | tf_op jit(solution)/shard_map/ppermute | solution.py:52
  128.4 3.0 %collective-permute-start.5 = (bf16[4,128,512]{2,1,0:T(8,128)(2,1)S(1)}, bf16[4,128,512]{2,1,0:T(8,128)(2,1)S(1)}, u32[]{:S(2)}, u32[]{:S(2)}) collective-permute-start(bf16[4,128,512]{2,1,0:T(8,128)(2,1)S(1)} %collective-permute-done.3), channel_id=1, source_target_pairs={{0,2},{2,4},{4,6},{6,8},{8,10},{10,12},{12,14},{14,16},{16,18},{18... | collective-permute-start | bytes 1572872 | tf_op jit(solution)/shard_map/ppermute | solution.py:52
  137.0 2.9 %collective-permute-done.5 = bf16[4,128,512]{2,1,0:T(8,128)(2,1)S(1)} collective-permute-done((bf16[4,128,512]{2,1,0:T(8,128)(2,1)S(1)}, bf16[4,128,512]{2,1,0:T(8,128)(2,1)S(1)}, u32[]{:S(2)}, u32[]{:S(2)}) %collective-permute-start.5) | collective-permute-done | bytes 524320 | tf_op jit(solution)/shard_map/ppermute | solution.py:52
  139.8 4.5 %collective-permute-start.7 = (bf16[4,128,512]{2,1,0:T(8,128)(2,1)S(1)}, bf16[4,128,512]{2,1,0:T(8,128)(2,1)S(1)}, u32[]{:S(2)}, u32[]{:S(2)}) collective-permute-start(bf16[4,128,512]{2,1,0:T(8,128)(2,1)S(1)} %collective-permute-done.5), channel_id=1, source_target_pairs={{0,2},{2,4},{4,6},{6,8},{8,10},{10,12},{12,14},{14,16},{16,18},{18... | collective-permute-start | bytes 1572872 | tf_op jit(solution)/shard_map/ppermute | solution.py:52
  149.9 2.8 %collective-permute-done.7 = bf16[4,128,512]{2,1,0:T(8,128)(2,1)S(1)} collective-permute-done((bf16[4,128,512]{2,1,0:T(8,128)(2,1)S(1)}, bf16[4,128,512]{2,1,0:T(8,128)(2,1)S(1)}, u32[]{:S(2)}, u32[]{:S(2)}) %collective-permute-start.7) | collective-permute-done | bytes 524320 | tf_op jit(solution)/shard_map/ppermute | solution.py:52
  152.8 5.8 %collective-permute-start.9 = (bf16[4,128,512]{2,1,0:T(8,128)(2,1)S(1)}, bf16[4,128,512]{2,1,0:T(8,128)(2,1)S(1)}, u32[]{:S(2)}, u32[]{:S(2)}) collective-permute-start(bf16[4,128,512]{2,1,0:T(8,128)(2,1)S(1)} %collective-permute-done.7), channel_id=1, source_target_pairs={{0,2},{2,4},{4,6},{6,8},{8,10},{10,12},{12,14},{14,16},{16,18},{18... | collective-permute-start | bytes 1572872 | tf_op jit(solution)/shard_map/ppermute | solution.py:52
  164.1 2.8 %collective-permute-done.9 = bf16[4,128,512]{2,1,0:T(8,128)(2,1)S(1)} collective-permute-done((bf16[4,128,512]{2,1,0:T(8,128)(2,1)S(1)}, bf16[4,128,512]{2,1,0:T(8,128)(2,1)S(1)}, u32[]{:S(2)}, u32[]{:S(2)}) %collective-permute-start.9) | collective-permute-done | bytes 524320 | tf_op jit(solution)/shard_map/ppermute | solution.py:52
  167.2 5.6 %collective-permute-start.10 = (bf16[4,128,512]{2,1,0:T(8,128)(2,1)S(1)}, bf16[4,128,512]{2,1,0:T(8,128)(2,1)S(1)}, u32[]{:S(2)}, u32[]{:S(2)}) collective-permute-start(bf16[4,128,512]{2,1,0:T(8,128)(2,1)S(1)} %collective-permute-done.8), channel_id=1, source_target_pairs={{0,30},{2,0},{4,2},{6,4},{8,6},{10,8},{12,10},{14,12},{16,14},{18,... | collective-permute-start | bytes 1572872 | tf_op jit(solution)/shard_map/ppermute | solution.py:54
  176.8 2.7 %collective-permute-done.11 = bf16[4,128,512]{2,1,0:T(8,128)(2,1)S(1)} collective-permute-done((bf16[4,128,512]{2,1,0:T(8,128)(2,1)S(1)}, bf16[4,128,512]{2,1,0:T(8,128)(2,1)S(1)}, u32[]{:S(2)}, u32[]{:S(2)}) %collective-permute-start.11) | collective-permute-done | bytes 524320 | tf_op jit(solution)/shard_map/ppermute | solution.py:52
  179.5 7.5 %collective-permute-start.13 = (bf16[4,128,512]{2,1,0:T(8,128)(2,1)S(1)}, bf16[4,128,512]{2,1,0:T(8,128)(2,1)S(1)}, u32[]{:S(2)}, u32[]{:S(2)}) collective-permute-start(bf16[4,128,512]{2,1,0:T(8,128)(2,1)S(1)} %collective-permute-done.11), channel_id=1, source_target_pairs={{0,2},{2,4},{4,6},{6,8},{8,10},{10,12},{12,14},{14,16},{16,18},{18... | collective-permute-start | bytes 1572872 | tf_op jit(solution)/shard_map/ppermute | solution.py:52
  191.1 2.6 %collective-permute-done.13 = bf16[4,128,512]{2,1,0:T(8,128)(2,1)S(1)} collective-permute-done((bf16[4,128,512]{2,1,0:T(8,128)(2,1)S(1)}, bf16[4,128,512]{2,1,0:T(8,128)(2,1)S(1)}, u32[]{:S(2)}, u32[]{:S(2)}) %collective-permute-start.13) | collective-permute-done | bytes 524320 | tf_op jit(solution)/shard_map/ppermute | solution.py:52
  193.7 7.5 %collective-permute-start.14 = (bf16[4,128,512]{2,1,0:T(8,128)(2,1)S(1)}, bf16[4,128,512]{2,1,0:T(8,128)(2,1)S(1)}, u32[]{:S(2)}, u32[]{:S(2)}) collective-permute-start(bf16[4,128,512]{2,1,0:T(8,128)(2,1)S(1)} %collective-permute-done.13), channel_id=1, source_target_pairs={{0,2},{2,4},{4,6},{6,8},{8,10},{10,12},{12,14},{14,16},{16,18},{18... | collective-permute-start | bytes 1572872 | tf_op jit(solution)/shard_map/ppermute | solution.py:52
  203.2 2.0 fusion.72
  209.6 10.6 %all-to-all-start.1 = ((bf16[4,16,8,384]{3,2,0,1:T(8,128)(2,1)}), bf16[4,16,8,384]{3,2,0,1:T(8,128)(2,1)S(1)}, u32[]{:S(2)}, u32[]{:S(2)}) async-start(bf16[4,16,8,384]{3,2,0,1:T(8,128)(2,1)} %copy.22), calls=%async_computation.1 | async-start | bytes 786432 | tf_op jit(solution)/shard_map/all_to_all | solution.py:75
  220.4 12.1 %all-to-all-done.1 = bf16[4,16,8,384]{3,2,0,1:T(8,128)(2,1)S(1)} async-done(((bf16[4,16,8,384]{3,2,0,1:T(8,128)(2,1)}), bf16[4,16,8,384]{3,2,0,1:T(8,128)(2,1)S(1)}, u32[]{:S(2)}, u32[]{:S(2)}) %all-to-all-start.1) | async-done | bytes 393248 | tf_op jit(solution)/shard_map/all_to_all | solution.py:75
  233.5 3.5 %all-to-all-start.2 = ((bf16[4,8,2,3072]{3,1,0,2:T(8,128)(2,1)}), bf16[4,8,2,3072]{3,1,0,2:T(8,128)(2,1)S(1)}, u32[]{:S(2)}, u32[]{:S(2)}) async-start(bf16[4,8,2,3072]{3,1,0,2:T(8,128)(2,1)} %copy.24), calls=%async_computation.2 | async-start | bytes 786432 | tf_op jit(solution)/shard_map/all_to_all | solution.py:79
  237.4 6.6 %all-to-all-done.2 = bf16[4,8,2,3072]{3,1,0,2:T(8,128)(2,1)S(1)} async-done(((bf16[4,8,2,3072]{3,1,0,2:T(8,128)(2,1)}), bf16[4,8,2,3072]{3,1,0,2:T(8,128)(2,1)S(1)}, u32[]{:S(2)}, u32[]{:S(2)}) %all-to-all-start.2) | async-done | bytes 393248 | tf_op jit(solution)/shard_map/all_to_all | solution.py:79
  (58 shorter events, 44.1 us)
Async XLA Ops:
  6.5 1.7 copy-start
  6.5 75.4 %all-gather.2.cloned.1.call-start = ((), (), s32[]{:S(2)}) async-start(), calls=%async_computation.3 | async-start | bytes 6684672 | tf_op jit(solution)/shard_map/all_gather | solution.py:36
  81.9 11.9 %copy-start.2 = (bf16[4,128,6144]{2,1,0:T(8,128)(2,1)S(1)}, bf16[4,128,6144]{2,1,0:T(8,128)(2,1)}, u32[]{:S(2)}) copy-start(bf16[4,128,6144]{2,1,0:T(8,128)(2,1)} %all-gather.2.cloned.1.call-done) | copy-start | bytes 18874372
  105.6 11.5 %collective-permute-start.1 = (bf16[4,128,512]{2,1,0:T(8,128)(2,1)S(1)}, bf16[4,128,512]{2,1,0:T(8,128)(2,1)S(1)}, u32[]{:S(2)}, u32[]{:S(2)}) collective-permute-start(bf16[4,128,512]{2,1,0:T(8,128)(2,1)S(1)} %fusion.78), channel_id=1, source_target_pairs={{0,2},{2,4},{4,6},{6,8},{8,10},{10,12},{12,14},{14,16},{16,18},{18... | collective-permute-start | bytes 1572872 | tf_op jit(solution)/shard_map/ppermute | solution.py:52
  105.9 12.2 %collective-permute-start = (bf16[4,128,512]{2,1,0:T(8,128)(2,1)S(1)}, bf16[4,128,512]{2,1,0:T(8,128)(2,1)S(1)}, u32[]{:S(2)}, u32[]{:S(2)}) collective-permute-start(bf16[4,128,512]{2,1,0:T(8,128)(2,1)S(1)} %fusion.78), channel_id=1, source_target_pairs={{0,30},{2,0},{4,2},{6,4},{8,6},{10,8},{12,10},{14,12},{16,14},{18,... | collective-permute-start | bytes 1572872 | tf_op jit(solution)/shard_map/ppermute | solution.py:54
  117.0 11.4 %collective-permute-start.3 = (bf16[4,128,512]{2,1,0:T(8,128)(2,1)S(1)}, bf16[4,128,512]{2,1,0:T(8,128)(2,1)S(1)}, u32[]{:S(2)}, u32[]{:S(2)}) collective-permute-start(bf16[4,128,512]{2,1,0:T(8,128)(2,1)S(1)} %collective-permute-done.1), channel_id=1, source_target_pairs={{0,2},{2,4},{4,6},{6,8},{8,10},{10,12},{12,14},{14,16},{16,18},{18... | collective-permute-start | bytes 1572872 | tf_op jit(solution)/shard_map/ppermute | solution.py:52
  118.0 13.4 %collective-permute-start.2 = (bf16[4,128,512]{2,1,0:T(8,128)(2,1)S(1)}, bf16[4,128,512]{2,1,0:T(8,128)(2,1)S(1)}, u32[]{:S(2)}, u32[]{:S(2)}) collective-permute-start(bf16[4,128,512]{2,1,0:T(8,128)(2,1)S(1)} %collective-permute-done), channel_id=1, source_target_pairs={{0,30},{2,0},{4,2},{6,4},{8,6},{10,8},{12,10},{14,12},{16,14},{18,... | collective-permute-start | bytes 1572872 | tf_op jit(solution)/shard_map/ppermute | solution.py:54
  125.5 94.7 %copy-start.3 = (f32[16,2]{0,1:T(2,128)S(1)}, f32[16,2]{0,1:T(2,128)}, u32[]{:S(2)}) copy-start(f32[16,2]{0,1:T(2,128)} %param.8) | copy-start | bytes 388
  128.4 11.4 %collective-permute-start.5 = (bf16[4,128,512]{2,1,0:T(8,128)(2,1)S(1)}, bf16[4,128,512]{2,1,0:T(8,128)(2,1)S(1)}, u32[]{:S(2)}, u32[]{:S(2)}) collective-permute-start(bf16[4,128,512]{2,1,0:T(8,128)(2,1)S(1)} %collective-permute-done.3), channel_id=1, source_target_pairs={{0,2},{2,4},{4,6},{6,8},{8,10},{10,12},{12,14},{14,16},{16,18},{18... | collective-permute-start | bytes 1572872 | tf_op jit(solution)/shard_map/ppermute | solution.py:52
  131.4 12.9 %collective-permute-start.4 = (bf16[4,128,512]{2,1,0:T(8,128)(2,1)S(1)}, bf16[4,128,512]{2,1,0:T(8,128)(2,1)S(1)}, u32[]{:S(2)}, u32[]{:S(2)}) collective-permute-start(bf16[4,128,512]{2,1,0:T(8,128)(2,1)S(1)} %collective-permute-done.2), channel_id=1, source_target_pairs={{0,30},{2,0},{4,2},{6,4},{8,6},{10,8},{12,10},{14,12},{16,14},{18,... | collective-permute-start | bytes 1572872 | tf_op jit(solution)/shard_map/ppermute | solution.py:54
  132.9 112.3 %copy-start.1 = (bf16[16,3072]{1,0:T(8,128)(2,1)S(1)}, bf16[16,3072]{1,0:T(8,128)(2,1)}, u32[]{:S(2)}) copy-start(bf16[16,3072]{1,0:T(8,128)(2,1)} %param.6) | copy-start | bytes 294916
  139.8 12.9 %collective-permute-start.7 = (bf16[4,128,512]{2,1,0:T(8,128)(2,1)S(1)}, bf16[4,128,512]{2,1,0:T(8,128)(2,1)S(1)}, u32[]{:S(2)}, u32[]{:S(2)}) collective-permute-start(bf16[4,128,512]{2,1,0:T(8,128)(2,1)S(1)} %collective-permute-done.5), channel_id=1, source_target_pairs={{0,2},{2,4},{4,6},{6,8},{8,10},{10,12},{12,14},{14,16},{16,18},{18... | collective-permute-start | bytes 1572872 | tf_op jit(solution)/shard_map/ppermute | solution.py:52
  144.3 14.2 %collective-permute-start.6 = (bf16[4,128,512]{2,1,0:T(8,128)(2,1)S(1)}, bf16[4,128,512]{2,1,0:T(8,128)(2,1)S(1)}, u32[]{:S(2)}, u32[]{:S(2)}) collective-permute-start(bf16[4,128,512]{2,1,0:T(8,128)(2,1)S(1)} %collective-permute-done.4), channel_id=1, source_target_pairs={{0,30},{2,0},{4,2},{6,4},{8,6},{10,8},{12,10},{14,12},{16,14},{18,... | collective-permute-start | bytes 1572872 | tf_op jit(solution)/shard_map/ppermute | solution.py:54
  152.8 14.2 %collective-permute-start.9 = (bf16[4,128,512]{2,1,0:T(8,128)(2,1)S(1)}, bf16[4,128,512]{2,1,0:T(8,128)(2,1)S(1)}, u32[]{:S(2)}, u32[]{:S(2)}) collective-permute-start(bf16[4,128,512]{2,1,0:T(8,128)(2,1)S(1)} %collective-permute-done.7), channel_id=1, source_target_pairs={{0,2},{2,4},{4,6},{6,8},{8,10},{10,12},{12,14},{14,16},{16,18},{18... | collective-permute-start | bytes 1572872 | tf_op jit(solution)/shard_map/ppermute | solution.py:52
  158.6 8.6 %collective-permute-start.8 = (bf16[4,128,512]{2,1,0:T(8,128)(2,1)S(1)}, bf16[4,128,512]{2,1,0:T(8,128)(2,1)S(1)}, u32[]{:S(2)}, u32[]{:S(2)}) collective-permute-start(bf16[4,128,512]{2,1,0:T(8,128)(2,1)S(1)} %collective-permute-done.6), channel_id=1, source_target_pairs={{0,30},{2,0},{4,2},{6,4},{8,6},{10,8},{12,10},{14,12},{16,14},{18,... | collective-permute-start | bytes 1572872 | tf_op jit(solution)/shard_map/ppermute | solution.py:54
  167.0 12.5 %collective-permute-start.11 = (bf16[4,128,512]{2,1,0:T(8,128)(2,1)S(1)}, bf16[4,128,512]{2,1,0:T(8,128)(2,1)S(1)}, u32[]{:S(2)}, u32[]{:S(2)}) collective-permute-start(bf16[4,128,512]{2,1,0:T(8,128)(2,1)S(1)} %collective-permute-done.9), channel_id=1, source_target_pairs={{0,2},{2,4},{4,6},{6,8},{8,10},{10,12},{12,14},{14,16},{16,18},{18... | collective-permute-start | bytes 1572872 | tf_op jit(solution)/shard_map/ppermute | solution.py:52
  167.2 19.8 %collective-permute-start.10 = (bf16[4,128,512]{2,1,0:T(8,128)(2,1)S(1)}, bf16[4,128,512]{2,1,0:T(8,128)(2,1)S(1)}, u32[]{:S(2)}, u32[]{:S(2)}) collective-permute-start(bf16[4,128,512]{2,1,0:T(8,128)(2,1)S(1)} %collective-permute-done.8), channel_id=1, source_target_pairs={{0,30},{2,0},{4,2},{6,4},{8,6},{10,8},{12,10},{14,12},{16,14},{18,... | collective-permute-start | bytes 1572872 | tf_op jit(solution)/shard_map/ppermute | solution.py:54
  179.5 14.2 %collective-permute-start.13 = (bf16[4,128,512]{2,1,0:T(8,128)(2,1)S(1)}, bf16[4,128,512]{2,1,0:T(8,128)(2,1)S(1)}, u32[]{:S(2)}, u32[]{:S(2)}) collective-permute-start(bf16[4,128,512]{2,1,0:T(8,128)(2,1)S(1)} %collective-permute-done.11), channel_id=1, source_target_pairs={{0,2},{2,4},{4,6},{6,8},{8,10},{10,12},{12,14},{14,16},{16,18},{18... | collective-permute-start | bytes 1572872 | tf_op jit(solution)/shard_map/ppermute | solution.py:52
  187.0 16.2 %collective-permute-start.12 = (bf16[4,128,512]{2,1,0:T(8,128)(2,1)S(1)}, bf16[4,128,512]{2,1,0:T(8,128)(2,1)S(1)}, u32[]{:S(2)}, u32[]{:S(2)}) collective-permute-start(bf16[4,128,512]{2,1,0:T(8,128)(2,1)S(1)} %collective-permute-done.10), channel_id=1, source_target_pairs={{0,30},{2,0},{4,2},{6,4},{8,6},{10,8},{12,10},{14,12},{16,14},{18,... | collective-permute-start | bytes 1572872 | tf_op jit(solution)/shard_map/ppermute | solution.py:54
  193.7 13.1 %collective-permute-start.14 = (bf16[4,128,512]{2,1,0:T(8,128)(2,1)S(1)}, bf16[4,128,512]{2,1,0:T(8,128)(2,1)S(1)}, u32[]{:S(2)}, u32[]{:S(2)}) collective-permute-start(bf16[4,128,512]{2,1,0:T(8,128)(2,1)S(1)} %collective-permute-done.13), channel_id=1, source_target_pairs={{0,2},{2,4},{4,6},{6,8},{8,10},{10,12},{12,14},{14,16},{16,18},{18... | collective-permute-start | bytes 1572872 | tf_op jit(solution)/shard_map/ppermute | solution.py:52
  209.6 22.8 %all-to-all-start.1 = ((bf16[4,16,8,384]{3,2,0,1:T(8,128)(2,1)}), bf16[4,16,8,384]{3,2,0,1:T(8,128)(2,1)S(1)}, u32[]{:S(2)}, u32[]{:S(2)}) async-start(bf16[4,16,8,384]{3,2,0,1:T(8,128)(2,1)} %copy.22), calls=%async_computation.1 | async-start | bytes 786432 | tf_op jit(solution)/shard_map/all_to_all | solution.py:75
  233.5 10.6 %all-to-all-start.2 = ((bf16[4,8,2,3072]{3,1,0,2:T(8,128)(2,1)}), bf16[4,8,2,3072]{3,1,0,2:T(8,128)(2,1)S(1)}, u32[]{:S(2)}, u32[]{:S(2)}) async-start(bf16[4,8,2,3072]{3,1,0,2:T(8,128)(2,1)} %copy.24), calls=%async_computation.2 | async-start | bytes 786432 | tf_op jit(solution)/shard_map/all_to_all | solution.py:79
Sparse Core Ops, SparseCore 0:
  20.0 61.8 all-gather.1
